TPU v7x, 512 devices: a whole 4x4x16 slice. The times are simulated.
512 devices in a mesh: dp: 64 (over x, z), head: 8 (over y, core).
Axes of the slice: x: 4, y: 4, z: 16, core: 2. Of those that a mesh axis runs over, the one named last changes fastest.
Arguments:
- gradients: float32 [3, 32, 64, 65536], P(None, 'head', None, 'dp'), may hold values from -0.6777015 to 0.6777015
- preconditioner: float32 [3, 32, 64, 64], P(None, 'head'), may hold values from -0.75 to 0.75
- partners: int32 [256, 7], P('dp'), may hold values from -1 to 255, as said below
Outputs:
- tiles: float32 [256, 256, 7, 256], P('head', 'dp')
Inputs may be any that keep to these rules, and one draw needn't show every extreme that they name: `partners`: blocks fall into clusters of consecutive blocks, each of at most 8 blocks; row a lists the blocks after a in its cluster in ascending order (slot k holds a + k + 1), then -1 in the remaining slots, so every unordered pair of distinct blocks of a cluster appears once. Some block has all 7 slots filled.
All inputs are finite; a program needn't handle non-finite values.
Results may differ from a plain program's by a relative error of at most 0.013.
Values may be sent and summed in bfloat16 or wider, within the bound.
A program may use at most 64 MiB of HBM per device.

v0:
```python
import jax
import jax.numpy as jnp
from jax import lax
from jax.sharding import PartitionSpec as P


def from_behind(array, axis, by):
    devices = lax.axis_size(axis)
    pairs = [(i, i + by) for i in range(devices) if 0 <= i + by < devices]
    return lax.ppermute(array, axis, pairs)


def cut_along(array, dim, devices):
    lengths = array.shape
    pieces = array.reshape(*lengths[:dim], devices, lengths[dim] // devices, *lengths[dim + 1 :])
    return jnp.moveaxis(pieces, dim, 0)


def summed_on_arrival(array, axis, dim):
    pieces = cut_along(array, dim, lax.axis_size(axis))
    arrived = lax.all_to_all(pieces, axis, split_axis=0, concat_axis=0, tiled=True)
    return arrived.astype(jnp.float32).sum(axis=0)


def per_device(gradients, preconditioner, partners):
    layers, head_count, head_depth, local_examples = gradients.shape
    group_rows = layers * head_count * head_depth
    block_total = partners.shape[0]
    reach_slots = partners.shape[1]
    block_size = local_examples // block_total
    scaled = jnp.einsum(
        "lhde,lhdn->lhen", preconditioner, gradients, precision=lax.Precision.HIGHEST
    )
    scaled = scaled.reshape(group_rows, local_examples).astype(jnp.bfloat16)
    plain_low = gradients.reshape(group_rows, local_examples).astype(jnp.bfloat16)
    pieces = []
    needed = reach_slots
    current = plain_low
    while needed > 0:
        take_blocks = min(block_total, needed)
        current = from_behind(current[:, : take_blocks * block_size], "dp", -1)
        pieces.append(current)
        needed = needed - take_blocks
    window = jnp.concatenate([plain_low] + pieces, axis=1)
    live_slot = (partners >= 0).astype(jnp.float32)
    scaled_blocks = scaled.reshape(group_rows, block_total, block_size)
    row_list = []
    for member in range(block_total):
        partner_cols = window[
            :, (member + 1) * block_size : (member + 1 + reach_slots) * block_size
        ]
        product = lax.dot_general(
            scaled_blocks[:, member, :],
            partner_cols,
            (((0,), (0,)), ((), ())),
            preferred_element_type=jnp.float32,
        )
        row_list.append(
            product.reshape(
                block_size // lax.axis_size("head") * lax.axis_size("head"), reach_slots, block_size
            )
            * live_slot[member][None, :, None]
        )
    return summed_on_arrival(jnp.stack(row_list, axis=1).astype(jnp.bfloat16), "head", 0)


def solution(mesh):
    in_specs = (P(None, "head", None, "dp"), P(None, "head", None, None), P("dp", None))
    out_specs = P("head", "dp", None, None)
    return jax.shard_map(
        per_device, mesh=mesh, in_specs=in_specs, out_specs=out_specs, check_vma=False
    )
```

profile of v0, /device:TPU:6, one launch (start us, length us, event | category | flops | bytes accessed | tf_op | source)
XLA Modules:
  0.0 140.2 jit_solution(18279026069613249159)
XLA Ops:
  0.0 0.0 copy-start
  0.0 2.2 %convert_element_type.23 = bf16[3,4,64,1024]{3,2,1,0:T(8,128)(2,1)S(1)} convert(f32[3,4,64,1024]{3,2,1,0:T(8,128)} %param.3) | non-fusion elementwise | flops 786432 | bytes 4718592 | tf_op jit(solution)/shard_map/convert_element_type | solution.py:35
  2.2 0.7 copy.15
  2.9 11.7 %collective-permute-start = (bf16[768,1024]{0,1:T(8,128)(2,1)S(1)}, bf16[768,1024]{0,1:T(8,128)(2,1)S(1)}, u32[]{:S(2)}, u32[]{:S(2)}) collective-permute-start(bf16[768,1024]{0,1:T(8,128)(2,1)S(1)} %copy.15), channel_id=1, source_target_pairs={{8,0},{16,8},{24,16},{32,24},{40,32},{48,40},{56,48},{64,56},{72,6... | collective-permute-start | bytes 4718600 | tf_op jit(solution)/shard_map/ppermute | solution.py:10
  14.6 33.6 %collective-permute-done = bf16[768,1024]{0,1:T(8,128)(2,1)S(1)} collective-permute-done((bf16[768,1024]{0,1:T(8,128)(2,1)S(1)}, bf16[768,1024]{0,1:T(8,128)(2,1)S(1)}, u32[]{:S(2)}, u32[]{:S(2)}) %collective-permute-start) | collective-permute-done | bytes 1572896 | tf_op jit(solution)/shard_map/ppermute | solution.py:10
  48.2 0.0 copy-start.1
  48.2 1.2 slice.53
  49.4 6.5 %collective-permute-start.1 = (bf16[768,768]{0,1:T(8,128)(2,1)}, bf16[768,768]{0,1:T(8,128)(2,1)}, u32[]{:S(2)}, u32[]{:S(2)}) collective-permute-start(bf16[768,768]{0,1:T(8,128)(2,1)} %slice.53), channel_id=1, source_target_pairs={{8,0},{16,8},{24,16},{32,24},{40,32},{48,40},{56,48},{64,56},{72,6... | collective-permute-start | bytes 3538952 | tf_op jit(solution)/shard_map/ppermute | solution.py:10
  55.9 0.0 copy-done.1
  55.9 0.0 copy-done
  55.9 5.8 %convolution_convert_fusion = bf16[3,4,64,1024]{3,2,1,0:T(8,128)(2,1)} fusion(f32[3,4,64,64]{3,2,1,0:T(8,128)S(1)} %copy-done, f32[3,4,64,1024]{3,2,1,0:T(8,128)} %param.3), kind=kOutput, calls=%fused_computation.9 | convolution fusion | flops 604766208 | bytes 4915200 | tf_op jit(solution)/shard_map/lhde,lhdn->lhen/dot_general | solution.py:31
  61.7 2.9 %convert_element_type.22 = bf16[768,4,256]{2,1,0:T(4,128)(2,1)S(1)} reshape(bf16[3,4,64,1024]{3,2,1,0:T(8,128)(2,1)} %convolution_convert_fusion) | data formatting | bytes 3145728 | tf_op jit(solution)/shard_map/convert_element_type | solution.py:34
  64.6 3.5 %fusion.5 = (bf16[768,1,256]{2,1,0:T(2,128)(2,1)}, bf16[768,1,256]{2,1,0:T(2,128)(2,1)}, bf16[768,1,256]{2,1,0:T(2,128)(2,1)}, bf16[768,1,256]{2,1,0:T(2,128)(2,1)}) fusion(bf16[768,4,256]{2,1,0:T(4,128)(2,1)S(1)} %convert_element_type.22), kind=kLoop, calls=%fused_computation.20 | loop fusion | bytes 3145728 | tf_op jit(solution)/shard_map/slice | solution.py:53
  68.1 0.0 copy-start.7
  68.1 0.0 copy-start.2
  68.2 3.0 %copy.30 = bf16[768,1,256]{0,2,1:T(8,128)(2,1)} copy(bf16[768,1,256]{2,1,0:T(2,128)(2,1)} %get-tuple-element.9) | data formatting | bytes 786432
  71.2 2.9 %copy.31 = bf16[768,1,256]{0,2,1:T(8,128)(2,1)} copy(bf16[768,1,256]{2,1,0:T(2,128)(2,1)} %get-tuple-element.8) | data formatting | bytes 786432
  74.1 2.9 %copy.32 = bf16[768,1,256]{0,2,1:T(8,128)(2,1)} copy(bf16[768,1,256]{2,1,0:T(2,128)(2,1)} %get-tuple-element.10) | data formatting | bytes 786432
  76.9 2.8 %copy.29 = bf16[768,1,256]{0,2,1:T(8,128)(2,1)} copy(bf16[768,1,256]{2,1,0:T(2,128)(2,1)} %get-tuple-element.7) | data formatting | bytes 786432
  79.7 0.0 copy-done.7
  79.8 0.8 collective-permute-done.1
  80.6 0.0 copy-done.2
  80.6 1.5 %pad_maximum_fusion = bf16[768,2816]{0,1:T(8,128)(2,1)S(1)} fusion(bf16[768,768]{0,1:T(8,128)(2,1)} %collective-permute-done.1, bf16[768,1024]{0,1:T(8,128)(2,1)S(1)} %copy-done.2, bf16[768,1024]{0,1:T(8,128)(2,1)S(1)} %copy.15), kind=kLoop, calls=%fused_computation.1 | loop fusion | flops 12976128 | bytes 8650752 | tf_op jit(solution)/shard_map/concatenate | solution.py:44
  82.1 0.0 copy-start.6
  82.1 0.4 fusion.4
  82.5 0.0 copy-start.5
  82.5 0.6 copy-done.6
  83.1 0.9 multiply_convert_fusion.2
  84.0 0.0 copy-done.5
  84.0 0.9 multiply_convert_fusion.1
  84.9 0.0 copy-start.4
  85.0 1.7 %pad_maximum_fusion.2 = (bf16[768,1792]{0,1:T(8,128)(2,1)S(1)}, bf16[768,1792]{0,1:T(8,128)(2,1)S(1)}) fusion(bf16[768,1024]{0,1:T(8,128)(2,1)S(1)} %copy-done.2, bf16[768,1024]{0,1:T(8,128)(2,1)S(1)} %copy.15, bf16[768,768]{0,1:T(8,128)(2,1)} %collective-permute-done.1), kind=kLoop, calls=%fused_computation.3 | loop fusion | flops 11010048 | bytes 9830400 | tf_op jit(solution)/shard_map/concatenate | solution.py:44
  86.7 0.0 copy-start.3
  86.7 0.0 copy-done.4
  86.7 0.9 multiply_convert_fusion
  87.6 0.1 copy-done.3
  87.7 0.9 multiply_convert_fusion.3
  88.6 0.5 pad_maximum_fusion.1
  89.1 0.5 copy.27
  89.7 48.3 %all_to_all.5 = bf16[8,32,4,7,256]{4,1,3,2,0:T(8,128)(2,1)S(1)} all-to-all(bf16[8,32,4,7,256]{4,1,3,2,0:T(8,128)(2,1)S(1)} %copy.27), channel_id=1, replica_groups=mesh['dp'=64,'head'=8] {'head'}, dimensions={0} | all-to-all | bytes 7340032 | tf_op jit(solution)/shard_map/all_to_all | solution.py:21
  138.0 0.7 convert_reduce_fusion
  138.7 1.5 %copy.25 = f32[32,4,7,256]{3,1,2,0:T(4,128)} copy(f32[32,4,7,256]{3,0,2,1:T(8,128)S(1)} %convert_reduce_fusion) | data formatting | bytes 1835008 | tf_op jit(solution)/shard_map/reduce_sum | solution.py:22
  (2 shorter events, 0.0 us)
Async XLA Ops:
  0.0 55.9 %copy-start = (f32[3,4,64,64]{3,2,1,0:T(8,128)S(1)}, f32[3,4,64,64]{3,2,1,0:T(8,128)}, u32[]{:S(2)}) copy-start(f32[3,4,64,64]{3,2,1,0:T(8,128)} %param.4) | copy-start | bytes 589828
  2.9 45.3 %collective-permute-start = (bf16[768,1024]{0,1:T(8,128)(2,1)S(1)}, bf16[768,1024]{0,1:T(8,128)(2,1)S(1)}, u32[]{:S(2)}, u32[]{:S(2)}) collective-permute-start(bf16[768,1024]{0,1:T(8,128)(2,1)S(1)} %copy.15), channel_id=1, source_target_pairs={{8,0},{16,8},{24,16},{32,24},{40,32},{48,40},{56,48},{64,56},{72,6... | collective-permute-start | bytes 4718600 | tf_op jit(solution)/shard_map/ppermute | solution.py:10
  48.2 7.7 %copy-start.1 = (bf16[768,1024]{0,1:T(8,128)(2,1)}, bf16[768,1024]{0,1:T(8,128)(2,1)S(1)}, u32[]{:S(2)}) copy-start(bf16[768,1024]{0,1:T(8,128)(2,1)S(1)} %collective-permute-done) | copy-start | bytes 4718596
  49.4 31.2 %collective-permute-start.1 = (bf16[768,768]{0,1:T(8,128)(2,1)}, bf16[768,768]{0,1:T(8,128)(2,1)}, u32[]{:S(2)}, u32[]{:S(2)}) collective-permute-start(bf16[768,768]{0,1:T(8,128)(2,1)} %slice.53), channel_id=1, source_target_pairs={{8,0},{16,8},{24,16},{32,24},{40,32},{48,40},{56,48},{64,56},{72,6... | collective-permute-start | bytes 3538952 | tf_op jit(solution)/shard_map/ppermute | solution.py:10
  68.1 11.6 %copy-start.7 = (s32[4,7]{1,0:T(4,128)S(1)}, s32[4,7]{1,0:T(4,128)}, u32[]{:S(2)}) copy-start(s32[4,7]{1,0:T(4,128)} %param.5) | copy-start | bytes 340
  68.1 12.4 %copy-start.2 = (bf16[768,1024]{0,1:T(8,128)(2,1)S(1)}, bf16[768,1024]{0,1:T(8,128)(2,1)}, u32[]{:S(2)}) copy-start(bf16[768,1024]{0,1:T(8,128)(2,1)} %copy-done.1) | copy-start | bytes 4718596
  82.1 1.0 copy-start.6
  82.5 1.5 %copy-start.5 = (bf16[768,1,256]{0,2,1:T(8,128)(2,1)S(1)}, bf16[768,1,256]{0,2,1:T(8,128)(2,1)}, u32[]{:S(2)}) copy-start(bf16[768,1,256]{0,2,1:T(8,128)(2,1)} %copy.31) | copy-start | bytes 1179652
  84.9 1.8 %copy-start.4 = (bf16[768,1,256]{0,2,1:T(8,128)(2,1)S(1)}, bf16[768,1,256]{0,2,1:T(8,128)(2,1)}, u32[]{:S(2)}) copy-start(bf16[768,1,256]{0,2,1:T(8,128)(2,1)} %copy.32) | copy-start | bytes 1179652
  86.7 1.0 copy-start.3
where the time goes:
time: 141 us; the launch traced here: 140 us
  blocking collectives  48.3 us (34%)
  waiting for transfers between devices  34.4 us (24%)
  local copies, waits for them, and re-layouts  23 us (16%)
  starting transfers between devices  18.2 us (13%)
  matrix products  9.49 us (7%)
  other arithmetic  6.65 us (5%)
    all_to_all x1, blocking collectives, summed_on_arrival(): lax.all_to_all(pieces, axis, split_axis=0, concat_axis=0, tiled=True)  48.3 us
    ppermute x2, waiting for transfers between devices, from_behind(): return lax.ppermute(array, axis, pairs)  34.4 us
    ppermute x2, starting transfers between devices, from_behind(): return lax.ppermute(array, axis, pairs)  18.2 us
    unnamed x20, local copies, waits for them, and re-layouts  12.3 us
    dot_general x1, matrix products, per_device(): jnp.einsum('lhde,lhdn->lhen', preconditioner, gradients, precision=lax.Pr...  5.84 us
    dot_general x4, matrix products, per_device(): lax.dot_general(scaled_blocks[:, member, :], partner_cols, (((0,), (0,)),...  3.66 us
    slice x1, local copies, waits for them, and re-layouts, per_device(): scaled_blocks[:, member, :]  3.5 us
    concatenate x2, other arithmetic, per_device(): window = jnp.concatenate([plain_low] + pieces, axis=1)  3.25 us
  transfers between devices with their start and end apart: 2, of which 2 were waited for; matrix products, arithmetic and copies ran while one was open for 17% of the time, Pallas kernels for 0%

commit v1 on v0

v1 whole, which is shorter than its diff:
```python
import functools

import jax
import jax.numpy as jnp
from jax import lax
from jax.experimental import pallas as pl
from jax.experimental.pallas import tpu as pltpu
from jax.sharding import PartitionSpec as P

MESH = pl.DeviceIdType.MESH
BF16 = jnp.bfloat16
F32 = jnp.float32

BS = 256
NB = 4
SLOTS = 7
ROWS = 768
LAYERS = 3
LROWS = ROWS // LAYERS
HD = 64
NY = 4
HALF = BS // 2
PIECE = HALF // NY

STAGES = (
    (tuple(("own", a, b) for b in range(1, NB) for a in range(b)), BS),
    (tuple(("own", a, 4) for a in range(NB)), BS),
    (
        tuple(("own", a, 5) for a in range(NB))
        + (("far", 3, 0), ("far", 2, 0), ("far", 3, 1), ("far", 2, 1)),
        BS,
    ),
    (tuple(("own", a, 6) for a in range(NB)) + (("far", 1, 0), ("far", 3, 2)), BS),
    (tuple(("own", a, 7) for a in range(NB)), BS // 2),
    (tuple(("own", a, 7) for a in range(NB)), BS // 2),
)
COLUMN0 = (0, 0, 0, 0, 0, BS // 2)
NSTAGE = len(STAGES)


def kernel(g_hbm, p_ref, out_ref, *scratch):
    (gbuf, plain, scaled, from_next, from_next_half, from_prev, ship0, ship1, far0, far1) = scratch[:10]
    stage_refs = [scratch[10 + 5 * s : 15 + 5 * s] for s in range(NSTAGE)]
    (
        load_sem,
        left_send,
        left_recv,
        right_send,
        right_recv,
        core_send,
        core_recv,
        y_send,
        y_recv,
        far_send,
        far_recv,
    ) = scratch[10 + 5 * NSTAGE :]
    ships, fars = {2: ship0, 3: ship1}, {2: far0, 3: far1}

    n_dp = lax.axis_size("dp")
    dp = lax.axis_index("dp")
    head = lax.axis_index("head")
    core = lax.rem(head, 2)
    y = lax.div(head, 2)
    previous = lax.rem(dp + n_dp - 1, n_dp)
    following = lax.rem(dp + 1, n_dp)
    other = head + 1 - 2 * core
    peers = [lax.rem(y + d, NY) * 2 + core for d in range(1, NY)]

    loads = []
    for j in range(NB):
        load = pltpu.make_async_copy(g_hbm.at[:, pl.ds(j * BS, BS)], gbuf.at[j], load_sem.at[j])
        load.start()
        loads.append(load)

    barrier = pltpu.get_barrier_semaphore()
    for target in (previous, following):
        pl.semaphore_signal(barrier, inc=1, device_id={"dp": target}, device_id_type=MESH)
    for target in [other] + peers:
        pl.semaphore_signal(barrier, inc=1, device_id={"head": target}, device_id_type=MESH)

    pending = []

    def send(src, dst, send_sem, recv_sem, device):
        copy = pltpu.make_async_remote_copy(
            src_ref=src,
            dst_ref=dst,
            send_sem=send_sem,
            recv_sem=recv_sem,
            device_id=device,
            device_id_type=MESH,
        )
        copy.start()
        pending.append(copy)
        return copy

    left = []
    for j in range(NB):
        loads[j].wait()
        plain[j] = gbuf[j].astype(BF16)
        if j == 0:
            pl.semaphore_wait(barrier, 2 + 1 + len(peers))
        if j < NB - 1:
            left.append(
                send(plain.at[j], from_next.at[j], left_send.at[j], left_recv.at[j], {"dp": previous})
            )
        else:
            for h in range(2):
                left.append(
                    send(
                        plain.at[j, :, pl.ds(h * HALF, HALF)],
                        from_next_half.at[h],
                        left_send.at[j + h],
                        left_recv.at[j + h],
                        {"dp": previous},
                    )
                )

    row_head = lax.broadcasted_iota(jnp.int32, (LROWS, LROWS), 0) // HD
    col_head = lax.broadcasted_iota(jnp.int32, (LROWS, LROWS), 1) // HD
    diagonal = (row_head == col_head).astype(F32)
    factors = []
    for layer in range(LAYERS):
        wide = jnp.concatenate([p_ref[pl.ds(layer * LROWS, LROWS), :]] * (LROWS // HD), axis=1)
        wide = (wide * diagonal).T
        high = wide.astype(BF16)
        factors.append((high, (wide - high.astype(F32)).astype(BF16)))
    right = {}
    for a in (3, 2, 1, 0):
        for layer in range(LAYERS):
            rows = pl.ds(layer * LROWS, LROWS)
            high = plain[a, rows, :]
            low = (gbuf[a, rows, :] - high.astype(F32)).astype(BF16)
            p_high, p_low = factors[layer]
            value = (
                jnp.dot(p_high, high, preferred_element_type=F32)
                + jnp.dot(p_low, high, preferred_element_type=F32)
                + jnp.dot(p_high, low, preferred_element_type=F32)
            )
            value = value.T.astype(BF16)
            for yy in range(NY):
                for cc in range(2):
                    scaled[cc, a, pl.ds(yy * PIECE, PIECE), pl.ds(layer * LROWS, LROWS)] = value[
                        (yy * 2 + cc) * PIECE : (yy * 2 + cc + 1) * PIECE
                    ]
        if a > 0:
            right[a] = send(
                scaled.at[:, a], from_prev.at[a - 1], right_send.at[a - 1], right_recv.at[a - 1], {"dp": following}
            )

    def columns_of(s, b):
        if b < NB:
            return plain[b]
        if b < 2 * NB - 1:
            return from_next[b - NB]
        return from_next_half[s - 4]

    core_copies, y_copies, far_copies = {}, {}, {}

    def compute(s):
        tiles, _ = STAGES[s]
        keep, outgoing, incoming, _, _ = stage_refs[s]
        index = 0
        while index < len(tiles):
            kind, a, b = tiles[index]
            count = 1
            if kind == "own":
                while index + count < len(tiles) and tiles[index + count] == ("own", a + count, b):
                    count += 1
            columns = columns_of(s, b) if kind == "own" else from_next[b]
            width = columns.shape[1]
            for which, ref in ((core, keep), (1 - core, outgoing)):
                if kind == "own":
                    lhs = scaled[which, a : a + count].reshape(count * HALF, ROWS)
                else:
                    lhs = from_prev[a - 1, which]
                product = jnp.dot(lhs, columns, preferred_element_type=F32)
                ref[index : index + count] = product.reshape(count, HALF, width).astype(ref.dtype)
            index += count
        core_copies[s] = send(outgoing, incoming, core_send.at[s], core_recv.at[s], {"head": other})

    def presum(s):
        tiles, width = STAGES[s]
        keep, _, incoming, pieces, arrived = stage_refs[s]
        core_copies[s].wait_recv()
        total = (keep[...] + incoming[...].astype(F32)).astype(BF16)
        for yy in range(NY):
            pieces[yy] = total[:, yy * PIECE : (yy + 1) * PIECE, :]
        y_copies[s] = []
        for d in range(1, NY):
            y_copies[s].append(
                send(
                    pieces.at[lax.rem(y + d, NY)],
                    arrived.at[d - 1],
                    y_send.at[s, d - 1],
                    y_recv.at[s, d - 1],
                    {"head": peers[d - 1]},
                )
            )

    def final(s):
        tiles, width = STAGES[s]
        keep, _, incoming, _, arrived = stage_refs[s]
        for copy in y_copies[s]:
            copy.wait_recv()
        mine = pl.ds(pl.multiple_of(y * PIECE, PIECE), PIECE)
        sent = 0
        for t, (kind, a, b) in enumerate(tiles):
            value = keep[t, mine, :] + incoming[t, mine, :].astype(F32)
            for d in range(NY - 1):
                value = value + arrived[d, t].astype(F32)
            if kind == "own":
                out_ref[:, b - a - 1, a, pl.ds(COLUMN0[s], width)] = value
            else:
                ships[s][sent] = value.astype(BF16)
                sent += 1
        if sent:
            far_copies[s] = send(ships[s], fars[s], far_send.at[s - 2], far_recv.at[s - 2], {"dp": previous})

    compute(0)
    presum(0)
    left[0].wait_recv()
    compute(1)
    presum(1)
    final(0)
    left[1].wait_recv()
    right[3].wait_recv()
    right[2].wait_recv()
    compute(2)
    presum(2)
    final(1)
    left[2].wait_recv()
    right[1].wait_recv()
    compute(3)
    presum(3)
    final(2)
    final(3)
    left[3].wait_recv()
    compute(4)
    presum(4)
    left[4].wait_recv()
    compute(5)
    presum(5)
    for s in (2, 3):
        far_copies[s].wait_recv()
        sent = 0
        for kind, a, c in STAGES[s][0]:
            if kind == "far":
                out_ref[:, 2 * NB + c - a - 1, a, :] = fars[s][sent].astype(F32)
                sent += 1
    final(4)
    final(5)
    for copy in pending:
        copy.wait_send()


def influence(gradients, preconditioner):
    scratch = [
        pltpu.VMEM((NB, ROWS, BS), F32),
        pltpu.VMEM((NB, ROWS, BS), BF16),
        pltpu.VMEM((2, NB, HALF, ROWS), BF16),
        pltpu.VMEM((NB - 1, ROWS, BS), BF16),
        pltpu.VMEM((2, ROWS, HALF), BF16),
        pltpu.VMEM((NB - 1, 2, HALF, ROWS), BF16),
        pltpu.VMEM((4, PIECE, BS), BF16),
        pltpu.VMEM((2, PIECE, BS), BF16),
        pltpu.VMEM((4, PIECE, BS), BF16),
        pltpu.VMEM((2, PIECE, BS), BF16),
    ]
    for tiles, width in STAGES:
        n = len(tiles)
        scratch += [
            pltpu.VMEM((n, HALF, width), F32),
            pltpu.VMEM((n, HALF, width), BF16),
            pltpu.VMEM((n, HALF, width), BF16),
            pltpu.VMEM((NY, n, PIECE, width), BF16),
            pltpu.VMEM((NY - 1, n, PIECE, width), BF16),
        ]
    dma = pltpu.SemaphoreType.DMA
    scratch += [
        dma((NB,)),
        dma((NB + 1,)),
        dma((NB + 1,)),
        dma((NB - 1,)),
        dma((NB - 1,)),
        dma((NSTAGE,)),
        dma((NSTAGE,)),
        dma((NSTAGE, NY - 1)),
        dma((NSTAGE, NY - 1)),
        dma((2,)),
        dma((2,)),
    ]
    return pl.pallas_call(
        kernel,
        out_shape=jax.ShapeDtypeStruct((PIECE, SLOTS, NB, BS), F32),
        in_specs=[pl.BlockSpec(memory_space=pltpu.HBM), pl.BlockSpec(memory_space=pltpu.VMEM)],
        out_specs=pl.BlockSpec(memory_space=pltpu.VMEM),
        scratch_shapes=scratch,
        compiler_params=pltpu.CompilerParams(
            collective_id=0, has_side_effects=True, vmem_limit_bytes=61 * 1024 * 1024
        ),
    )(gradients, preconditioner)


def per_device(gradients, preconditioner, partners):
    tiles = influence(gradients.reshape(ROWS, NB * BS), preconditioner.reshape(ROWS, HD))
    live = (partners >= 0).astype(F32)
    return (tiles * live.T[None, :, :, None]).transpose(0, 2, 1, 3)


def solution(mesh):
    in_specs = (P(None, "head", None, "dp"), P(None, "head", None, None), P("dp", None))
    out_specs = P("head", "dp", None, None)
    return jax.shard_map(
        per_device, mesh=mesh, in_specs=in_specs, out_specs=out_specs, check_vma=False
    )
```

time: 141 us -> 65 us (0.46)
  the two profiles are of different devices: /device:TPU:6 before, /device:TPU:1 now
where the time goes in v1:
time: 65 us; the launch traced here: 64.8 us
  Pallas kernels  61.7 us (95%)
  other arithmetic  3.01 us (5%)
    pallas_call x1, Pallas kernels, influence(): pl.pallas_call(kernel, out_shape=jax.ShapeDtypeStruct((PIECE, SLOTS, NB,...  61.7 us
    transpose x2, other arithmetic, per_device(): return (tiles * live.T[None, :, :, None]).transpose(0, 2, 1, 3)  3.01 us

profile of v1, /device:TPU:1, one launch (start us, length us, event | category | flops | bytes accessed | tf_op | source)
XLA Modules:
  0.0 64.8 jit_solution(3866362617386340674)
XLA Ops:
  0.0 0.7 %convert_bitcast_fusion = f32[7,4]{0,1:T(4,128)S(1)} fusion(s32[4,7]{1,0:T(4,128)} %param.5), kind=kLoop, calls=%fused_computation.1 | loop fusion | flops 56 | bytes 224 | tf_op jit(solution)/shard_map/transpose | solution.py:307
  0.7 0.1 copy.4
  0.8 61.7 %shard_map.37 = f32[32,7,4,256]{3,2,1,0:T(4,128)} custom-call(f32[768,1024]{1,0:T(8,128)} %bitcast.6, f32[768,64]{1,0:T(8,128)} %bitcast.7), custom_call_target="tpu_custom_call" | custom-call | tf_op jit(solution)/shard_map/pallas_call | solution.py:292
  62.5 2.3 %multiply_bitcast_fusion = f32[32,4,7,256]{3,1,2,0:T(4,128)} fusion(f32[32,7,4,256]{3,2,1,0:T(4,128)} %shard_map.37, f32[7,4]{1,0:T(8,128)S(1)} %copy.4), kind=kLoop, calls=%fused_computation | loop fusion | flops 229376 | bytes 1835120 | tf_op jit(solution)/shard_map/transpose | solution.py:307

commit v2 on v1

v2 whole, which is shorter than its diff:
```python
import jax
import jax.numpy as jnp
from jax import lax
from jax.experimental import pallas as pl
from jax.experimental.pallas import tpu as pltpu
from jax.sharding import PartitionSpec as P

MESH = pl.DeviceIdType.MESH
BF16 = jnp.bfloat16
F32 = jnp.float32

BS = 256
NB = 4
SLOTS = 7
ROWS = 768
LAYERS = 3
LROWS = ROWS // LAYERS
HD = 64
NY = 4
HALF = BS // 2
PIECE = HALF // NY
KH = ROWS // 2
LIVE_ROWS = 32
LANES = 128

STAGES = (
    tuple(("own", a, b) for b in range(1, NB) for a in range(b)),
    tuple(("fold", a, 0) for a in range(NB)),
    tuple(("fold", a, 1) for a in range(NB)),
    tuple(("fold", a, 2) for a in range(NB)),
    tuple(("fold", a, 3) for a in range(NB)) + (("far", 1, 0),),
    tuple(("far", 3, c) for c in range(3)) + tuple(("relay", 3, c) for c in range(3)),
    (("far", 2, 0), ("far", 2, 1)),
)
NSTAGE = len(STAGES)
ONE_BACK = ("fold", "far")
SHIP1 = [sum(kind in ONE_BACK for kind, _, _ in tiles) for tiles in STAGES]
RELAY_STAGE = 5
RX, RA2 = 4, 5


def kernel(g_hbm, p_ref, partners_ref, out_ref, *scratch):
    it = iter(scratch)
    take = lambda n: [next(it) for _ in range(n)]
    gbuf, plain, scaled, from_next, from_prev, left_mix, right_mix = take(7)
    live0, live1, live2 = take(3)
    ship2, got2 = take(2)
    stage_refs = [take(4) for _ in range(NSTAGE)]
    ship_refs = [take(2) if n else None for n in SHIP1]
    (load_sem, live_send, live_recv, left_send, left_recv, right_send, right_recv) = take(7)
    (core_send, core_recv, y_send, y_recv, ship_send, ship_recv) = take(6)

    n_dp = lax.axis_size("dp")
    dp = lax.axis_index("dp")
    head = lax.axis_index("head")
    core = lax.rem(head, 2)
    y = lax.div(head, 2)
    before, before2 = [lax.rem(dp + n_dp - d, n_dp) for d in (1, 2)]
    after, after2 = [lax.rem(dp + d, n_dp) for d in (1, 2)]
    other = head + 1 - 2 * core
    peers = [lax.rem(y + d, NY) * 2 + core for d in range(1, NY)]

    loads = {}
    for j in (0, 3, 1, 2):
        load = pltpu.make_async_copy(g_hbm.at[:, pl.ds(j * BS, BS)], gbuf.at[j], load_sem.at[j])
        load.start()
        loads[j] = load

    barrier = pltpu.get_barrier_semaphore()
    neighbours = (before, after, before2, after2)
    for target in neighbours:
        pl.semaphore_signal(barrier, inc=1, device_id={"dp": target}, device_id_type=MESH)
    for target in [other] + peers:
        pl.semaphore_signal(barrier, inc=1, device_id={"head": target}, device_id_type=MESH)

    pending = []

    def send(src, dst, send_sem, recv_sem, device):
        copy = pltpu.make_async_remote_copy(
            src_ref=src,
            dst_ref=dst,
            send_sem=send_sem,
            recv_sem=recv_sem,
            device_id=device,
            device_id_type=MESH,
        )
        copy.start()
        pending.append(copy)
        return copy

    live0[...] = jnp.zeros((LIVE_ROWS, LANES), F32)
    for a in range(NB):
        for k in range(SLOTS):
            slot = jnp.where(partners_ref[a, k] >= 0, 1.0, 0.0).astype(F32)
            live0[a * 8 + k : a * 8 + k + 1, :] = jnp.full((1, LANES), slot, F32)

    def live(ref, a, target, width=BS):
        row = a * 8 + target - a - 1
        return jnp.concatenate([ref[row : row + 1, :]] * (width // LANES), axis=1)

    def load_plain(j):
        loads[j].wait()
        plain[j] = gbuf[j].astype(BF16)

    left, right = {}, {}

    def send_left(n, src):
        left[n] = send(src, from_next.at[n], left_send.at[n], left_recv.at[n], {"dp": before})

    def send_right(n, src):
        right[n] = send(src, from_prev.at[n], right_send.at[n], right_recv.at[n], {"dp": after})

    a_rows, b_rows = pl.ds(0, KH), pl.ds(KH, KH)

    row_head = lax.broadcasted_iota(jnp.int32, (LROWS, LROWS), 0) // HD
    col_head = lax.broadcasted_iota(jnp.int32, (LROWS, LROWS), 1) // HD
    diagonal = (row_head == col_head).astype(F32)
    factors = []
    for layer in range(LAYERS):
        wide = jnp.concatenate([p_ref[pl.ds(layer * LROWS, LROWS), :]] * (LROWS // HD), axis=1)
        wide = (wide * diagonal).T
        high = wide.astype(BF16)
        factors.append((high, (wide - high.astype(F32)).astype(BF16)))

    def scale(a):
        for layer in range(LAYERS):
            rows = pl.ds(layer * LROWS, LROWS)
            high = plain[a, rows, :]
            low = (gbuf[a, rows, :] - high.astype(F32)).astype(BF16)
            p_high, p_low = factors[layer]
            value = (
                jnp.dot(p_high, high, preferred_element_type=F32)
                + jnp.dot(p_low, high, preferred_element_type=F32)
                + jnp.dot(p_high, low, preferred_element_type=F32)
            )
            value = value.T.astype(BF16)
            for yy in range(NY):
                for cc in range(2):
                    scaled[cc, a, pl.ds(yy * PIECE, PIECE), rows] = value[
                        (yy * 2 + cc) * PIECE : (yy * 2 + cc + 1) * PIECE
                    ]

    def either(flag, yes, no):
        return (flag * yes.astype(F32) + (1.0 - flag) * no.astype(F32)).astype(BF16)

    load_plain(0)
    pl.semaphore_wait(barrier, len(neighbours) + 1 + len(peers))
    send_left(0, plain.at[0, a_rows])
    live_copies = [
        send(live0, live1, live_send.at[0], live_recv.at[0], {"dp": after}),
        send(live0, live2, live_send.at[1], live_recv.at[1], {"dp": after2}),
    ]
    load_plain(3)
    scale(3)
    send_right(3, scaled.at[:, 3, :, b_rows])
    load_plain(1)
    send_left(1, plain.at[1, a_rows])
    scale(0)
    scale(1)
    reach = live(live0, 1, 8, KH)
    for cc in range(2):
        right_mix[0, cc] = either(reach, scaled[cc, 1, :, a_rows], scaled[cc, 0, :, b_rows])
    send_right(0, right_mix.at[0])
    send_right(1, scaled.at[:, 1, :, b_rows])
    load_plain(2)
    for copy in live_copies:
        copy.wait_recv()
    reach = live(live2, 2, 8)
    for n in (2, 3):
        left_mix[n - 2] = either(reach, plain[n - 2, b_rows, :], plain[n, a_rows, :])
        send_left(n, left_mix.at[n - 2])
    scale(2)
    send_right(2, scaled.at[:, 2, :, b_rows])

    core_copies, y_copies, ship_copies, ship2_copies = {}, {}, {}, {}

    def own_rows(a, count, columns):
        lhs = scaled[:, a : a + count, :, columns]
        return lhs.reshape(2 * count * HALF, lhs.shape[-1])

    def product(lhs, rhs):
        return jnp.dot(lhs, rhs, preferred_element_type=F32)

    def prev_rows(n):
        return from_prev[n].reshape(BS, KH)

    def compute(s):
        tiles = STAGES[s]
        tile, incoming, _, _ = stage_refs[s]
        if s == 0:
            index = 0
            for b in range(1, NB):
                value = product(own_rows(0, b, pl.ds(0, ROWS)), plain[b])
                tile[:, index : index + b] = value.reshape(2, b, HALF, BS).astype(BF16)
                index += b
        for index, (kind, a, n) in enumerate(tiles):
            if kind == "fold":
                if a == 0:
                    forward = product(own_rows(0, NB, a_rows), from_next[n]).reshape(2, NB, HALF, BS)
                value = forward[:, a] * live(live0, a, NB + n) + product(
                    prev_rows(n), plain[a, b_rows, :]
                ).reshape(2, HALF, BS) * live(live1, n, NB + a)
            elif kind == "far":
                value = product(prev_rows({1: 0, 2: RA2, 3: RX}[a]), from_next[n])
                if a < 3:
                    value = value + product(prev_rows(a), from_next[2 + n])
                value = value.reshape(2, HALF, BS) * live(live1, a, 2 * NB + n)
            elif kind == "relay":
                value = product(prev_rows(RX), plain[n, b_rows, :]).reshape(2, HALF, BS)
                value = value * live(live2, a, 2 * NB + n)
            if kind != "own":
                tile[:, index] = value.astype(BF16)
        core_copies[s] = send(tile.at[1 - core], incoming, core_send.at[s], core_recv.at[s], {"head": other})

    def presum(s):
        tile, incoming, pieces, arrived = stage_refs[s]
        core_copies[s].wait_recv()
        total = (tile[core].astype(F32) + incoming[...].astype(F32)).astype(BF16)
        for yy in range(NY):
            pieces[yy] = total[:, yy * PIECE : (yy + 1) * PIECE, :]
        y_copies[s] = [
            send(
                pieces.at[lax.rem(y + d, NY)],
                arrived.at[d - 1],
                y_send.at[s, d - 1],
                y_recv.at[s, d - 1],
                {"head": peers[d - 1]},
            )
            for d in range(1, NY)
        ]

    def final(s):
        tile, incoming, _, arrived = stage_refs[s]
        for copy in y_copies[s]:
            copy.wait_recv()
        mine = pl.ds(pl.multiple_of(y * PIECE, PIECE), PIECE)
        sent, sent2 = 0, 0
        for t, (kind, a, n) in enumerate(STAGES[s]):
            value = tile[core, t, mine, :].astype(F32) + incoming[t, mine, :].astype(F32)
            for d in range(NY - 1):
                value = value + arrived[d, t].astype(F32)
            if kind == "own":
                out_ref[:, n - a - 1, a, :] = value * live(live0, a, n)
            elif kind == "fold":
                out_ref[:, NB + n - a - 1, a, :] = value * live(live0, a, NB + n)
                ship_refs[s][0][sent] = (value * live(live1, n, NB + a)).astype(BF16)
                sent += 1
            elif kind == "far":
                ship_refs[s][0][sent] = value.astype(BF16)
                sent += 1
            else:
                ship2[sent2] = value.astype(BF16)
                sent2 += 1
        if sent2:
            ship2_copies[s] = send(ship2, got2, ship_send.at[NSTAGE], ship_recv.at[NSTAGE], {"dp": before2})
        if sent:
            ship_copies[s] = send(*ship_refs[s], ship_send.at[s], ship_recv.at[s], {"dp": before})

    def collect(s):
        if s in ship_copies:
            ship_copies[s].wait_recv()
        if s in ship2_copies:
            ship2_copies[s].wait_recv()
        got, got_far = 0, 0
        for kind, a, n in STAGES[s]:
            if kind == "fold":
                row, target = n, NB + a
                column = target - row - 1
                out_ref[:, column, row, :] = out_ref[:, column, row, :] + ship_refs[s][1][got].astype(F32)
                got += 1
            elif kind == "far":
                value = ship_refs[s][1][got].astype(F32)
                if a == 3:
                    value = value + got2[n].astype(F32)
                out_ref[:, 2 * NB + n - a - 1, a, :] = value
                got += 1

    compute(0)
    right[3].wait_recv()
    reach = live(live1, 3, 8, KH)
    for cc in range(2):
        right_mix[1, cc] = either(reach, from_prev[3, cc], scaled[cc, 3, :, a_rows])
    send_right(RX, right_mix.at[1])
    send_right(RA2, scaled.at[:, 2, :, a_rows])
    presum(0)
    left[0].wait_recv()
    right[0].wait_recv()
    compute(1)
    presum(1)
    final(0)
    left[1].wait_recv()
    right[1].wait_recv()
    compute(2)
    presum(2)
    final(1)
    left[2].wait_recv()
    right[2].wait_recv()
    compute(3)
    presum(3)
    final(2)
    left[3].wait_recv()
    compute(4)
    presum(4)
    final(3)
    right[RX].wait_recv()
    compute(5)
    presum(5)
    final(4)
    right[RA2].wait_recv()
    compute(6)
    presum(6)
    final(5)
    for s in range(1, 5):
        collect(s)
    final(6)
    collect(5)
    collect(6)
    for copy in pending:
        copy.wait_send()


def influence(gradients, preconditioner, partners):
    dma = pltpu.SemaphoreType.DMA
    scratch = [
        pltpu.VMEM((NB, ROWS, BS), F32),
        pltpu.VMEM((NB, ROWS, BS), BF16),
        pltpu.VMEM((2, NB, HALF, ROWS), BF16),
        pltpu.VMEM((NB, KH, BS), BF16),
        pltpu.VMEM((6, 2, HALF, KH), BF16),
        pltpu.VMEM((2, KH, BS), BF16),
        pltpu.VMEM((2, 2, HALF, KH), BF16),
        pltpu.VMEM((LIVE_ROWS, LANES), F32),
        pltpu.VMEM((LIVE_ROWS, LANES), F32),
        pltpu.VMEM((LIVE_ROWS, LANES), F32),
        pltpu.VMEM((3, PIECE, BS), BF16),
        pltpu.VMEM((3, PIECE, BS), BF16),
    ]
    for tiles in STAGES:
        n = len(tiles)
        scratch += [
            pltpu.VMEM((2, n, HALF, BS), BF16),
            pltpu.VMEM((n, HALF, BS), BF16),
            pltpu.VMEM((NY, n, PIECE, BS), BF16),
            pltpu.VMEM((NY - 1, n, PIECE, BS), BF16),
        ]
    for n in SHIP1:
        if n:
            scratch += [pltpu.VMEM((n, PIECE, BS), BF16)] * 2
    scratch += [
        dma((NB,)),
        dma((2,)),
        dma((2,)),
        dma((NB,)),
        dma((NB,)),
        dma((6,)),
        dma((6,)),
        dma((NSTAGE,)),
        dma((NSTAGE,)),
        dma((NSTAGE, NY - 1)),
        dma((NSTAGE, NY - 1)),
        dma((NSTAGE + 1,)),
        dma((NSTAGE + 1,)),
    ]
    return pl.pallas_call(
        kernel,
        out_shape=jax.ShapeDtypeStruct((PIECE, SLOTS, NB, BS), F32),
        in_specs=[
            pl.BlockSpec(memory_space=pltpu.HBM),
            pl.BlockSpec(memory_space=pltpu.VMEM),
            pl.BlockSpec(memory_space=pltpu.SMEM),
        ],
        out_specs=pl.BlockSpec(memory_space=pltpu.VMEM),
        scratch_shapes=scratch,
        compiler_params=pltpu.CompilerParams(
            collective_id=0, has_side_effects=True, vmem_limit_bytes=61 * 1024 * 1024
        ),
    )(gradients, preconditioner, partners)


def per_device(gradients, preconditioner, partners):
    tiles = influence(gradients.reshape(ROWS, NB * BS), preconditioner.reshape(ROWS, HD), partners)
    return tiles.transpose(0, 2, 1, 3)


def solution(mesh):
    in_specs = (P(None, "head", None, "dp"), P(None, "head", None, None), P("dp", None))
    out_specs = P("head", "dp", None, None)
    return jax.shard_map(
        per_device, mesh=mesh, in_specs=in_specs, out_specs=out_specs, check_vma=False
    )
```

time: 65 us -> 61.7 us (0.949)
  other arithmetic: 3.01 us -> 0 us
  Pallas kernels: 61.7 us -> 59.3 us
  local copies, waits for them, and re-layouts: 0.1 us -> 2.26 us
    transpose x2 -> x0, other arithmetic: 3.01 us -> none  [per_device(): return (tiles * live.T[None, :, :, None]).transpose(0, 2, 1, 3)]
    pallas_call x1, Pallas kernels: 61.7 us -> 59.3 us  [influence(): pl.pallas_call(kernel, out_shape=jax.ShapeDtypeStruct((PIECE, SLOTS, NB,...]
    unnamed x0 -> x1, local copies, waits for them, and re-layouts: none -> 2.26 us
where the time goes in v2:
time: 61.7 us; the launch traced here: 61.6 us
  Pallas kernels  59.3 us (96%)
  local copies, waits for them, and re-layouts  2.26 us (4%)
    pallas_call x1, Pallas kernels, influence(): pl.pallas_call(kernel, out_shape=jax.ShapeDtypeStruct((PIECE, SLOTS, NB,...  59.3 us
    unnamed x1, local copies, waits for them, and re-layouts  2.26 us

profile of v2, /device:TPU:1, one launch (start us, length us, event | category | flops | bytes accessed | tf_op | source)
XLA Modules:
  0.0 61.6 jit_solution(15644003080920347367)
XLA Ops:
  0.0 59.3 %shard_map.37 = f32[32,7,4,256]{3,2,1,0:T(4,128)} custom-call(f32[768,1024]{1,0:T(8,128)} %bitcast.4, f32[768,64]{1,0:T(8,128)} %bitcast.5, s32[4,7]{1,0:T(4,128)} %partners_ref.1), custom_call_target="tpu_custom_call" | custom-call | tf_op jit(solution)/shard_map/pallas_call | solution.py:364
  59.3 2.3 %copy.5 = f32[32,4,7,256]{3,1,2,0:T(4,128)} copy(f32[32,4,7,256]{3,1,2,0:T(4,128)} %bitcast.3) | data formatting | bytes 1835008

commit v3 on v2

v3 whole, which is shorter than its diff:
```python
import jax
import jax.numpy as jnp
from jax import lax
from jax.experimental import pallas as pl
from jax.experimental.pallas import tpu as pltpu
from jax.sharding import PartitionSpec as P

MESH = pl.DeviceIdType.MESH
BF16 = jnp.bfloat16
F32 = jnp.float32

BS = 256
NB = 4
SLOTS = 7
ROWS = 768
LAYERS = 3
LROWS = ROWS // LAYERS
HD = 64
NY = 4
HALF = BS // 2
PIECE = HALF // NY
KH = ROWS // 2
LIVE_ROWS = 32
LANES = 128

def fold(n):
    return tuple((("alpha", a, n), ("beta", n, a)) for a in range(NB))


STAGES = (
    tuple((("own", a, b),) for b in range(1, NB) for a in range(min(b, 2))),
    fold(0),
    fold(3),
    (
        (("far", 3, 0), ("relay", 3, 0)),
        (("far", 3, 1), ("relay", 3, 1)),
        (("own", 2, 3), ("relay", 3, 2)),
    ),
    fold(1),
    fold(2),
    (
        (("far", 2, 0), ("far", 3, 2)),
        (("far", 2, 1), ("far", 1, 0)),
    ),
)
NSTAGE = len(STAGES)
ONE_BACK = ("beta", "far")


def ship_terms(slot):
    return [term for term in slot if term[0] in ONE_BACK]


SHIP1 = [sum(len(ship_terms(slot)) > 0 for slot in slots) for slots in STAGES]
RX, RA2 = 4, 5


def kernel(g_hbm, p_hbm, partners_hbm, out_ref, *scratch):
    it = iter(scratch)
    take = lambda n: [next(it) for _ in range(n)]
    gbuf, pbuf, partners_smem, plain, scaled, from_next, from_prev, left_mix, right_mix = take(9)
    live0, live1, live2 = take(3)
    ship2, got2 = take(2)
    stage_refs = [take(4) for _ in range(NSTAGE)]
    ship_refs = [take(2) if n else None for n in SHIP1]
    (load_sem, live_send, live_recv, left_send, left_recv, right_send, right_recv) = take(7)
    (core_send, core_recv, y_send, y_recv, ship_send, ship_recv) = take(6)

    n_dp = lax.axis_size("dp")
    dp = lax.axis_index("dp")
    head = lax.axis_index("head")
    core = lax.rem(head, 2)
    y = lax.div(head, 2)
    before, before2 = [lax.rem(dp + n_dp - d, n_dp) for d in (1, 2)]
    after, after2 = [lax.rem(dp + d, n_dp) for d in (1, 2)]
    other = head + 1 - 2 * core
    peers = [lax.rem(y + d, NY) * 2 + core for d in range(1, NY)]

    barrier = pltpu.get_barrier_semaphore()
    neighbours = (before, after, before2, after2)
    for target in neighbours:
        pl.semaphore_signal(barrier, inc=1, device_id={"dp": target}, device_id_type=MESH)
    for target in [other] + peers:
        pl.semaphore_signal(barrier, inc=1, device_id={"head": target}, device_id_type=MESH)

    loads = {}
    for name, src, dst in [("p", p_hbm, pbuf)] + [
        (j, g_hbm.at[:, pl.ds(j * BS, BS)], gbuf.at[j]) for j in (3, 0, 1, 2)
    ] + [("partners", partners_hbm, partners_smem)]:
        load = pltpu.make_async_copy(src, dst, load_sem.at[len(loads)])
        load.start()
        loads[name] = load

    pending = []

    def send(src, dst, send_sem, recv_sem, device):
        copy = pltpu.make_async_remote_copy(
            src_ref=src,
            dst_ref=dst,
            send_sem=send_sem,
            recv_sem=recv_sem,
            device_id=device,
            device_id_type=MESH,
        )
        copy.start()
        pending.append(copy)
        return copy

    def live(ref, a, target, width=BS):
        row = a * 8 + target - a - 1
        return jnp.concatenate([ref[row : row + 1, :]] * (width // LANES), axis=1)

    def load_plain(j):
        loads[j].wait()
        plain[j] = gbuf[j].astype(BF16)

    left, right = {}, {}

    def send_left(n, src):
        left[n] = send(src, from_next.at[n], left_send.at[n], left_recv.at[n], {"dp": before})

    def send_right(n, src):
        right[n] = send(src, from_prev.at[n], right_send.at[n], right_recv.at[n], {"dp": after})

    a_rows, b_rows = pl.ds(0, KH), pl.ds(KH, KH)

    def scale(a):
        for layer in range(LAYERS):
            rows = pl.ds(layer * LROWS, LROWS)
            high = plain[a, rows, :]
            low = (gbuf[a, rows, :] - high.astype(F32)).astype(BF16)
            p_high, p_low = factors[layer]
            value = (
                jnp.dot(p_high, high, preferred_element_type=F32)
                + jnp.dot(p_low, high, preferred_element_type=F32)
                + jnp.dot(p_high, low, preferred_element_type=F32)
            )
            value = value.T.astype(BF16)
            for yy in range(NY):
                for cc in range(2):
                    scaled[cc, a, pl.ds(yy * PIECE, PIECE), rows] = value[
                        (yy * 2 + cc) * PIECE : (yy * 2 + cc + 1) * PIECE
                    ]

    def either(flag, yes, no):
        return (flag * yes.astype(F32) + (1.0 - flag) * no.astype(F32)).astype(BF16)

    row_head = lax.broadcasted_iota(jnp.int32, (LROWS, LROWS), 0) // HD
    col_head = lax.broadcasted_iota(jnp.int32, (LROWS, LROWS), 1) // HD
    diagonal = (row_head == col_head).astype(F32)
    loads["p"].wait()
    factors = []
    for layer in range(LAYERS):
        wide = jnp.concatenate([pbuf[pl.ds(layer * LROWS, LROWS), :]] * (LROWS // HD), axis=1)
        wide = (wide * diagonal).T
        high = wide.astype(BF16)
        factors.append((high, (wide - high.astype(F32)).astype(BF16)))

    load_plain(3)
    scale(3)
    load_plain(0)
    loads["partners"].wait()
    live0[...] = jnp.zeros((LIVE_ROWS, LANES), F32)
    for a in range(NB):
        for k in range(SLOTS):
            slot = jnp.where(partners_smem[a, k] >= 0, 1.0, 0.0).astype(F32)
            live0[a * 8 + k : a * 8 + k + 1, :] = jnp.full((1, LANES), slot, F32)

    pl.semaphore_wait(barrier, len(neighbours) + 1 + len(peers))
    live_copies = [
        send(live0, live1, live_send.at[0], live_recv.at[0], {"dp": after}),
        send(live0, live2, live_send.at[1], live_recv.at[1], {"dp": after2}),
    ]
    send_right(3, scaled.at[:, 3, :, b_rows])
    send_left(0, plain.at[0, a_rows])
    load_plain(1)
    send_left(1, plain.at[1, a_rows])
    scale(0)
    scale(1)
    reach = live(live0, 1, 8, KH)
    for cc in range(2):
        right_mix[0, cc] = either(reach, scaled[cc, 1, :, a_rows], scaled[cc, 0, :, b_rows])
    send_right(0, right_mix.at[0])
    load_plain(2)
    for copy in live_copies:
        copy.wait_recv()
    reach = live(live2, 2, 8)
    for n in (3, 2):
        left_mix[n - 2] = either(reach, plain[n - 2, b_rows, :], plain[n, a_rows, :])
        send_left(n, left_mix.at[n - 2])
    scale(2)

    core_copies, y_copies, ship_copies, ship2_copies = {}, {}, {}, {}

    def own_rows(a, count, columns):
        lhs = scaled[:, a : a + count, :, columns]
        return lhs.reshape(2 * count * HALF, lhs.shape[-1])

    def product(lhs, rhs):
        return jnp.dot(lhs, rhs, preferred_element_type=F32)

    def prev_rows(n):
        return from_prev[n].reshape(BS, KH)

    def part(kind, a, n, forward):
        if kind == "own":
            return product(own_rows(a, 1, pl.ds(0, ROWS)), plain[n]).reshape(2, HALF, BS) * live(live0, a, n)
        if kind == "alpha":
            return forward[:, a] * live(live0, a, NB + n)
        if kind == "beta":
            value = product(prev_rows(a), plain[n, b_rows, :])
            return value.reshape(2, HALF, BS) * live(live1, a, NB + n)
        if kind == "relay":
            value = product(prev_rows(RX), plain[n, b_rows, :])
            return value.reshape(2, HALF, BS) * live(live2, a, 2 * NB + n)
        value = product(prev_rows({1: 0, 2: RA2, 3: RX}[a]), from_next[n])
        if a < 3:
            value = value + product(prev_rows(a), from_next[2 + n])
        return value.reshape(2, HALF, BS) * live(live1, a, 2 * NB + n)

    def compute(s):
        tile, incoming, _, _ = stage_refs[s]
        if s == 0:
            index = 0
            for b in range(1, NB):
                count = min(b, 2)
                value = product(own_rows(0, count, pl.ds(0, ROWS)), plain[b])
                tile[:, index : index + count] = value.reshape(2, count, HALF, BS).astype(BF16)
                index += count
        else:
            forward = None
            if STAGES[s][0][0][0] == "alpha":
                n = STAGES[s][0][0][2]
                forward = product(own_rows(0, NB, a_rows), from_next[n]).reshape(2, NB, HALF, BS)
            for index, slot in enumerate(STAGES[s]):
                value = part(*slot[0], forward)
                for term in slot[1:]:
                    value = value + part(*term, forward)
                tile[:, index] = value.astype(BF16)
        core_copies[s] = send(tile.at[1 - core], incoming, core_send.at[s], core_recv.at[s], {"head": other})

    def presum(s):
        tile, incoming, pieces, arrived = stage_refs[s]
        core_copies[s].wait_recv()
        total = (tile[core].astype(F32) + incoming[...].astype(F32)).astype(BF16)
        for yy in range(NY):
            pieces[yy] = total[:, yy * PIECE : (yy + 1) * PIECE, :]
        y_copies[s] = [
            send(
                pieces.at[lax.rem(y + d, NY)],
                arrived.at[d - 1],
                y_send.at[s, d - 1],
                y_recv.at[s, d - 1],
                {"head": peers[d - 1]},
            )
            for d in range(1, NY)
        ]

    def final(s):
        tile, incoming, _, arrived = stage_refs[s]
        for copy in y_copies[s]:
            copy.wait_recv()
        mine = pl.ds(pl.multiple_of(y * PIECE, PIECE), PIECE)
        sent, sent2 = 0, 0
        for t, slot in enumerate(STAGES[s]):
            value = tile[core, t, mine, :].astype(F32) + incoming[t, mine, :].astype(F32)
            for d in range(NY - 1):
                value = value + arrived[d, t].astype(F32)
            for kind, a, n in slot:
                if kind == "own":
                    out_ref[:, n - a - 1, a, :] = value * live(live0, a, n)
                elif kind == "alpha":
                    out_ref[:, NB + n - a - 1, a, :] = value * live(live0, a, NB + n)
                elif kind == "relay":
                    ship2[sent2] = (value * live(live2, a, 2 * NB + n)).astype(BF16)
                    sent2 += 1
            flag = None
            for kind, a, n in ship_terms(slot):
                one = live(live1, a, (NB if kind == "beta" else 2 * NB) + n)
                flag = one if flag is None else flag + one
            if flag is not None:
                ship_refs[s][0][sent] = (value * flag).astype(BF16)
                sent += 1
        if sent2:
            ship2_copies[s] = send(ship2, got2, ship_send.at[NSTAGE], ship_recv.at[NSTAGE], {"dp": before2})
        if sent:
            ship_copies[s] = send(*ship_refs[s], ship_send.at[s], ship_recv.at[s], {"dp": before})

    def collect(s):
        if s in ship_copies:
            ship_copies[s].wait_recv()
        if s in ship2_copies:
            ship2_copies[s].wait_recv()
        got = 0
        for slot in STAGES[s]:
            for kind, a, n in ship_terms(slot):
                value = ship_refs[s][1][got].astype(F32)
                if kind == "beta":
                    column = NB + n - a - 1
                    out_ref[:, column, a, :] = out_ref[:, column, a, :] + value
                else:
                    value = value * live(live0, a, 2 * NB + n)
                    if a == 3:
                        value = value + got2[n].astype(F32)
                    out_ref[:, 2 * NB + n - a - 1, a, :] = value
            got += len(ship_terms(slot)) > 0

    compute(0)
    right[3].wait_recv()
    reach = live(live1, 3, 8, KH)
    for cc in range(2):
        right_mix[1, cc] = either(reach, from_prev[3, cc], scaled[cc, 3, :, a_rows])
    send_right(RX, right_mix.at[1])
    send_right(1, scaled.at[:, 1, :, b_rows])
    send_right(2, scaled.at[:, 2, :, b_rows])
    send_right(RA2, scaled.at[:, 2, :, a_rows])
    presum(0)
    left[0].wait_recv()
    right[0].wait_recv()
    compute(1)
    presum(1)
    left[1].wait_recv()
    left[3].wait_recv()
    compute(2)
    presum(2)
    final(0)
    right[RX].wait_recv()
    compute(3)
    presum(3)
    final(1)
    left[2].wait_recv()
    right[1].wait_recv()
    compute(4)
    presum(4)
    final(2)
    right[2].wait_recv()
    compute(5)
    presum(5)
    final(3)
    right[RA2].wait_recv()
    compute(6)
    presum(6)
    final(4)
    final(5)
    for s in range(1, 4):
        collect(s)
    final(6)
    for s in range(4, NSTAGE):
        collect(s)
    for copy in pending:
        copy.wait_send()


def influence(gradients, preconditioner, partners):
    dma = pltpu.SemaphoreType.DMA
    scratch = [
        pltpu.VMEM((NB, ROWS, BS), F32),
        pltpu.VMEM((ROWS, HD), F32),
        pltpu.SMEM((NB, SLOTS), jnp.int32),
        pltpu.VMEM((NB, ROWS, BS), BF16),
        pltpu.VMEM((2, NB, HALF, ROWS), BF16),
        pltpu.VMEM((NB, KH, BS), BF16),
        pltpu.VMEM((6, 2, HALF, KH), BF16),
        pltpu.VMEM((2, KH, BS), BF16),
        pltpu.VMEM((2, 2, HALF, KH), BF16),
        pltpu.VMEM((LIVE_ROWS, LANES), F32),
        pltpu.VMEM((LIVE_ROWS, LANES), F32),
        pltpu.VMEM((LIVE_ROWS, LANES), F32),
        pltpu.VMEM((3, PIECE, BS), BF16),
        pltpu.VMEM((3, PIECE, BS), BF16),
    ]
    for tiles in STAGES:
        n = len(tiles)
        scratch += [
            pltpu.VMEM((2, n, HALF, BS), BF16),
            pltpu.VMEM((n, HALF, BS), BF16),
            pltpu.VMEM((NY, n, PIECE, BS), BF16),
            pltpu.VMEM((NY - 1, n, PIECE, BS), BF16),
        ]
    for n in SHIP1:
        if n:
            scratch += [pltpu.VMEM((n, PIECE, BS), BF16)] * 2
    scratch += [
        dma((NB + 2,)),
        dma((2,)),
        dma((2,)),
        dma((NB,)),
        dma((NB,)),
        dma((6,)),
        dma((6,)),
        dma((NSTAGE,)),
        dma((NSTAGE,)),
        dma((NSTAGE, NY - 1)),
        dma((NSTAGE, NY - 1)),
        dma((NSTAGE + 1,)),
        dma((NSTAGE + 1,)),
    ]
    return pl.pallas_call(
        kernel,
        out_shape=jax.ShapeDtypeStruct((PIECE, SLOTS, NB, BS), F32),
        in_specs=[pl.BlockSpec(memory_space=pltpu.HBM)] * 3,
        out_specs=pl.BlockSpec(memory_space=pltpu.VMEM),
        scratch_shapes=scratch,
        compiler_params=pltpu.CompilerParams(
            collective_id=0, has_side_effects=True, vmem_limit_bytes=48 * 1024 * 1024
        ),
    )(*[pltpu.with_memory_space_constraint(x, pltpu.HBM) for x in (gradients, preconditioner, partners)])


def per_device(gradients, preconditioner, partners):
    tiles = influence(gradients.reshape(ROWS, NB * BS), preconditioner.reshape(ROWS, HD), partners)
    return tiles.transpose(0, 2, 1, 3)


def solution(mesh):
    in_specs = (P(None, "head", None, "dp"), P(None, "head", None, None), P("dp", None))
    out_specs = P("head", "dp", None, None)
    return jax.shard_map(
        per_device, mesh=mesh, in_specs=in_specs, out_specs=out_specs, check_vma=False
    )
```

time: 61.7 us -> 52.7 us (0.85)
  Pallas kernels: 59.3 us -> 51.7 us
  local copies, waits for them, and re-layouts: 2.26 us -> 0.93 us
    pallas_call x1, Pallas kernels: 59.3 us -> 51.7 us  [influence(): pl.pallas_call(kernel, out_shape=jax.ShapeDtypeStruct((PIECE, SLOTS, NB,...]
    unnamed x1, local copies, waits for them, and re-layouts: 2.26 us -> 0.93 us
where the time goes in v3:
time: 52.7 us; the launch traced here: 52.6 us
  Pallas kernels  51.7 us (98%)
  local copies, waits for them, and re-layouts  0.93 us (2%)
    pallas_call x1, Pallas kernels, influence(): pl.pallas_call(kernel, out_shape=jax.ShapeDtypeStruct((PIECE, SLOTS, NB,...  51.7 us

profile of v3, /device:TPU:1, one launch (start us, length us, event | category | flops | bytes accessed | tf_op | source)
XLA Modules:
  0.0 52.6 jit_solution(16743092259094282975)
XLA Ops:
  0.0 51.7 %shard_map.37 = f32[32,7,4,256]{3,2,1,0:T(4,128)S(1)} custom-call(f32[768,1024]{1,0:T(8,128)} %bitcast.4, f32[768,64]{1,0:T(8,128)} %bitcast.5, s32[4,7]{1,0:T(4,128)} %partners_hbm.1), custom_call_target="tpu_custom_call" | custom-call | tf_op jit(solution)/shard_map/pallas_call | solution.py:398
  51.7 0.9 %copy.5 = f32[32,4,7,256]{3,1,2,0:T(4,128)} copy(f32[32,4,7,256]{3,1,2,0:T(4,128)S(1)} %bitcast.3) | data formatting | bytes 1835008

commit v4 on v3

--- a/solution.py
+++ b/solution.py
@@ -28,20 +28,17 @@
 
 
 STAGES = (
-    tuple((("own", a, b),) for b in range(1, NB) for a in range(min(b, 2))),
+    tuple((("own", a, b),) for a, b in ((0, 1), (0, 2), (1, 2), (1, 3), (2, 3))),
     fold(0),
     fold(3),
-    (
-        (("far", 3, 0), ("relay", 3, 0)),
-        (("far", 3, 1), ("relay", 3, 1)),
-        (("own", 2, 3), ("relay", 3, 2)),
-    ),
     fold(1),
     fold(2),
     (
-        (("far", 2, 0), ("far", 3, 2)),
-        (("far", 2, 1), ("far", 1, 0)),
+        (("far", 3, 1), ("relay", 3, 0)),
+        (("far", 3, 2), ("relay", 3, 1), ("far", 2, 0)),
+        (("relay", 3, 2), ("far", 2, 1), ("far", 1, 0)),
     ),
+    ((("ahead", 1, 0),), (("ahead", 2, 0),), (("ahead", 3, 0), ("own", 0, 3))),
 )
 NSTAGE = len(STAGES)
 ONE_BACK = ("beta", "far")
@@ -52,13 +49,14 @@
 
 
 SHIP1 = [sum(len(ship_terms(slot)) > 0 for slot in slots) for slots in STAGES]
-RX, RA2 = 4, 5
+RX = LX = 4
+MIXED = 5
 
 
 def kernel(g_hbm, p_hbm, partners_hbm, out_ref, *scratch):
     it = iter(scratch)
     take = lambda n: [next(it) for _ in range(n)]
-    gbuf, pbuf, partners_smem, plain, scaled, from_next, from_prev, left_mix, right_mix = take(9)
+    gbuf, pbuf, partners_smem, plain, scaled, from_next, from_prev, left_mix, right_mix, early = take(10)
     live0, live1, live2 = take(3)
     ship2, got2 = take(2)
     stage_refs = [take(4) for _ in range(NSTAGE)]
@@ -84,9 +82,9 @@
         pl.semaphore_signal(barrier, inc=1, device_id={"head": target}, device_id_type=MESH)
 
     loads = {}
-    for name, src, dst in [("p", p_hbm, pbuf)] + [
-        (j, g_hbm.at[:, pl.ds(j * BS, BS)], gbuf.at[j]) for j in (3, 0, 1, 2)
-    ] + [("partners", partners_hbm, partners_smem)]:
+    blocks = [(j, g_hbm.at[:, pl.ds(j * BS, BS)], gbuf.at[j]) for j in (0, 2, 3, 1)]
+    tables = [("partners", partners_hbm, partners_smem), ("p", p_hbm, pbuf)]
+    for name, src, dst in tables + blocks:
         load = pltpu.make_async_copy(src, dst, load_sem.at[len(loads)])
         load.start()
         loads[name] = load
@@ -119,13 +117,14 @@
     def send_left(n, src):
         left[n] = send(src, from_next.at[n], left_send.at[n], left_recv.at[n], {"dp": before})
 
-    def send_right(n, src):
-        right[n] = send(src, from_prev.at[n], right_send.at[n], right_recv.at[n], {"dp": after})
+    def send_right(n, src, dst=None):
+        dst = from_prev.at[n] if dst is None else dst
+        right[n] = send(src, dst, right_send.at[n], right_recv.at[n], {"dp": after})
 
     a_rows, b_rows = pl.ds(0, KH), pl.ds(KH, KH)
 
-    def scale(a):
-        for layer in range(LAYERS):
+    def scale(a, layers=range(LAYERS)):
+        for layer in layers:
             rows = pl.ds(layer * LROWS, LROWS)
             high = plain[a, rows, :]
             low = (gbuf[a, rows, :] - high.astype(F32)).astype(BF16)
@@ -156,9 +155,6 @@
         high = wide.astype(BF16)
         factors.append((high, (wide - high.astype(F32)).astype(BF16)))
 
-    load_plain(3)
-    scale(3)
-    load_plain(0)
     loads["partners"].wait()
     live0[...] = jnp.zeros((LIVE_ROWS, LANES), F32)
     for a in range(NB):
@@ -166,29 +162,39 @@
             slot = jnp.where(partners_smem[a, k] >= 0, 1.0, 0.0).astype(F32)
             live0[a * 8 + k : a * 8 + k + 1, :] = jnp.full((1, LANES), slot, F32)
 
+    load_plain(0)
+    scale(0, (1, 2))
+    load_plain(2)
+    scale(2, (0, 1))
+    reach = live(live0, 2, 9, KH)
+    for cc in range(2):
+        right_mix[0, cc] = either(reach, scaled[cc, 2, :, a_rows], scaled[cc, 0, :, b_rows])
+
     pl.semaphore_wait(barrier, len(neighbours) + 1 + len(peers))
     live_copies = [
         send(live0, live1, live_send.at[0], live_recv.at[0], {"dp": after}),
         send(live0, live2, live_send.at[1], live_recv.at[1], {"dp": after2}),
     ]
+    send_right(0, right_mix.at[0])
+    send_left(0, plain.at[0, a_rows])
+    load_plain(3)
+    scale(3, (1, 2))
     send_right(3, scaled.at[:, 3, :, b_rows])
-    send_left(0, plain.at[0, a_rows])
     load_plain(1)
-    send_left(1, plain.at[1, a_rows])
-    scale(0)
-    scale(1)
-    reach = live(live0, 1, 8, KH)
-    for cc in range(2):
-        right_mix[0, cc] = either(reach, scaled[cc, 1, :, a_rows], scaled[cc, 0, :, b_rows])
-    send_right(0, right_mix.at[0])
-    load_plain(2)
+    scale(0, (0,))
+    scale(2, (2,))
+    scale(3, (0,))
     for copy in live_copies:
         copy.wait_recv()
     reach = live(live2, 2, 8)
     for n in (3, 2):
         left_mix[n - 2] = either(reach, plain[n - 2, b_rows, :], plain[n, a_rows, :])
-        send_left(n, left_mix.at[n - 2])
-    scale(2)
+    send_left(3, left_mix.at[1])
+    send_left(1, plain.at[1, a_rows])
+    send_left(2, left_mix.at[0])
+    scale(1)
+    send_right(1, scaled.at[:, 1, :, b_rows])
+    send_right(2, scaled.at[:, 2, :, b_rows])
 
     core_copies, y_copies, ship_copies, ship2_copies = {}, {}, {}, {}
 
@@ -202,42 +208,61 @@
     def prev_rows(n):
         return from_prev[n].reshape(BS, KH)
 
-    def part(kind, a, n, forward):
+    def flag_of(kind, a, n):
+        if kind == "relay":
+            return live(live2, a, 2 * NB + n)
+        if kind in ONE_BACK:
+            return live(live1, a, (NB if kind == "beta" else 2 * NB) + n)
+        return live(live0, a, {"own": 0, "alpha": NB, "ahead": 2 * NB}[kind] + n)
+
+    def beta(a, n):
+        return product(prev_rows(a), plain[n, b_rows, :]).reshape(2, HALF, BS) * flag_of("beta", a, n)
+
+    def far(a, n):
+        value = product(prev_rows(a), from_next[2 + n])
+        if n == 1:
+            value = value + product(prev_rows(0), from_next[n])
+        return value.reshape(2, HALF, BS) * flag_of("far", a, n)
+
+    def mixed_early():
+        early[:, 0] = far(2, 0)
+        early[:, 1] = far(2, 1) + far(1, 0)
+
+    def mixed(half):
+        tile = stage_refs[MIXED][0]
+        lhs = from_prev[RX, half]
+        for index, (c, n) in enumerate(((1, 0), (2, 1), (None, 2))):
+            value = product(lhs, plain[n, b_rows, :]) * flag_of("relay", 3, n)
+            if c is not None:
+                value = value + product(lhs, from_next[c]) * flag_of("far", 3, c)
+            if index:
+                value = value + early[half, index - 1]
+            tile[half, index] = value.astype(BF16)
+
+    def to_core(s):
+        tile, incoming, _, _ = stage_refs[s]
+        core_copies[s] = send(tile.at[1 - core], incoming, core_send.at[s], core_recv.at[s], {"head": other})
+
+    def compute(s):
+        tile = stage_refs[s][0]
+        kind, _, n = STAGES[s][0][0]
         if kind == "own":
-            return product(own_rows(a, 1, pl.ds(0, ROWS)), plain[n]).reshape(2, HALF, BS) * live(live0, a, n)
-        if kind == "alpha":
-            return forward[:, a] * live(live0, a, NB + n)
-        if kind == "beta":
-            value = product(prev_rows(a), plain[n, b_rows, :])
-            return value.reshape(2, HALF, BS) * live(live1, a, NB + n)
-        if kind == "relay":
-            value = product(prev_rows(RX), plain[n, b_rows, :])
-            return value.reshape(2, HALF, BS) * live(live2, a, 2 * NB + n)
-        value = product(prev_rows({1: 0, 2: RA2, 3: RX}[a]), from_next[n])
-        if a < 3:
-            value = value + product(prev_rows(a), from_next[2 + n])
-        return value.reshape(2, HALF, BS) * live(live1, a, 2 * NB + n)
-
-    def compute(s):
-        tile, incoming, _, _ = stage_refs[s]
-        if s == 0:
             index = 0
-            for b in range(1, NB):
-                count = min(b, 2)
-                value = product(own_rows(0, count, pl.ds(0, ROWS)), plain[b])
+            for b, first, count in ((1, 0, 1), (2, 0, 2), (3, 1, 2)):
+                value = product(own_rows(first, count, pl.ds(0, ROWS)), plain[b])
                 tile[:, index : index + count] = value.reshape(2, count, HALF, BS).astype(BF16)
                 index += count
+        elif kind == "ahead":
+            value = product(own_rows(1, NB - 1, a_rows), from_next[LX]).reshape(2, NB - 1, HALF, BS)
+            tile[:, 0:2] = value[:, 0:2].astype(BF16)
+            last = product(own_rows(0, 1, pl.ds(0, ROWS)), plain[3]).reshape(2, HALF, BS)
+            last = last * flag_of("own", 0, 3) + value[:, 2] * flag_of("ahead", 3, 0)
+            tile[:, 2] = last.astype(BF16)
         else:
-            forward = None
-            if STAGES[s][0][0][0] == "alpha":
-                n = STAGES[s][0][0][2]
-                forward = product(own_rows(0, NB, a_rows), from_next[n]).reshape(2, NB, HALF, BS)
-            for index, slot in enumerate(STAGES[s]):
-                value = part(*slot[0], forward)
-                for term in slot[1:]:
-                    value = value + part(*term, forward)
-                tile[:, index] = value.astype(BF16)
-        core_copies[s] = send(tile.at[1 - core], incoming, core_send.at[s], core_recv.at[s], {"head": other})
+            forward = product(own_rows(0, NB, a_rows), from_next[n]).reshape(2, NB, HALF, BS)
+            for a in range(NB):
+                tile[:, a] = (forward[:, a] * flag_of("alpha", a, n) + beta(n, a)).astype(BF16)
+        to_core(s)
 
     def presum(s):
         tile, incoming, pieces, arrived = stage_refs[s]
@@ -266,18 +291,18 @@
             value = tile[core, t, mine, :].astype(F32) + incoming[t, mine, :].astype(F32)
             for d in range(NY - 1):
                 value = value + arrived[d, t].astype(F32)
-            for kind, a, n in slot:
-                if kind == "own":
-                    out_ref[:, n - a - 1, a, :] = value * live(live0, a, n)
-                elif kind == "alpha":
-                    out_ref[:, NB + n - a - 1, a, :] = value * live(live0, a, NB + n)
+            flag = None
+            for term in slot:
+                kind, a, n = term
+                one = flag_of(*term)
+                if kind in ONE_BACK:
+                    flag = one if flag is None else flag + one
                 elif kind == "relay":
-                    ship2[sent2] = (value * live(live2, a, 2 * NB + n)).astype(BF16)
+                    ship2[n] = (value * one).astype(BF16)
                     sent2 += 1
-            flag = None
-            for kind, a, n in ship_terms(slot):
-                one = live(live1, a, (NB if kind == "beta" else 2 * NB) + n)
-                flag = one if flag is None else flag + one
+                else:
+                    target = {"own": 0, "alpha": NB, "ahead": 2 * NB}[kind] + n
+                    out_ref[:, target - a - 1, a, :] = value * one
             if flag is not None:
                 ship_refs[s][0][sent] = (value * flag).astype(BF16)
                 sent += 1
@@ -295,58 +320,64 @@
         for slot in STAGES[s]:
             for kind, a, n in ship_terms(slot):
                 value = ship_refs[s][1][got].astype(F32)
-                if kind == "beta":
-                    column = NB + n - a - 1
-                    out_ref[:, column, a, :] = out_ref[:, column, a, :] + value
-                else:
-                    value = value * live(live0, a, 2 * NB + n)
-                    if a == 3:
-                        value = value + got2[n].astype(F32)
-                    out_ref[:, 2 * NB + n - a - 1, a, :] = value
+                target = (NB if kind == "beta" else 2 * NB) + n
+                if kind == "far":
+                    value = value * live(live0, a, target)
+                if kind == "beta" or n == 0:
+                    value = value + out_ref[:, target - a - 1, a, :]
+                elif a == 3:
+                    value = value + got2[n].astype(F32)
+                out_ref[:, target - a - 1, a, :] = value
             got += len(ship_terms(slot)) > 0
+        if s in ship2_copies:
+            out_ref[:, 2 * NB - 4, 3, :] = out_ref[:, 2 * NB - 4, 3, :] + got2[0].astype(F32)
 
     compute(0)
+    presum(0)
+    left[0].wait_recv()
+    send_left(LX, from_next.at[0])
+    right[0].wait_recv()
+    compute(1)
+    presum(1)
     right[3].wait_recv()
     reach = live(live1, 3, 8, KH)
     for cc in range(2):
         right_mix[1, cc] = either(reach, from_prev[3, cc], scaled[cc, 3, :, a_rows])
-    send_right(RX, right_mix.at[1])
-    send_right(1, scaled.at[:, 1, :, b_rows])
-    send_right(2, scaled.at[:, 2, :, b_rows])
-    send_right(RA2, scaled.at[:, 2, :, a_rows])
-    presum(0)
-    left[0].wait_recv()
-    right[0].wait_recv()
-    compute(1)
-    presum(1)
-    left[1].wait_recv()
+    send_right(RX, right_mix.at[1, 1 - core], from_prev.at[RX, 1 - core])
+    send_right(RX + 1, right_mix.at[1, core], from_prev.at[RX, core])
     left[3].wait_recv()
     compute(2)
     presum(2)
     final(0)
-    right[RX].wait_recv()
+    left[1].wait_recv()
+    right[1].wait_recv()
     compute(3)
     presum(3)
     final(1)
     left[2].wait_recv()
-    right[1].wait_recv()
+    right[2].wait_recv()
     compute(4)
+    mixed_early()
     presum(4)
     final(2)
-    right[2].wait_recv()
-    compute(5)
+    right[RX].wait_recv()
+    mixed(1 - core)
+    to_core(MIXED)
+    final(3)
+    right[RX + 1].wait_recv()
+    mixed(core)
     presum(5)
-    final(3)
-    right[RA2].wait_recv()
+    left[LX].wait_recv()
     compute(6)
     presum(6)
     final(4)
+    collect(1)
+    collect(2)
     final(5)
-    for s in range(1, 4):
-        collect(s)
+    collect(3)
     final(6)
-    for s in range(4, NSTAGE):
-        collect(s)
+    collect(4)
+    collect(5)
     for copy in pending:
         copy.wait_send()
 
@@ -359,10 +390,11 @@
         pltpu.SMEM((NB, SLOTS), jnp.int32),
         pltpu.VMEM((NB, ROWS, BS), BF16),
         pltpu.VMEM((2, NB, HALF, ROWS), BF16),
-        pltpu.VMEM((NB, KH, BS), BF16),
-        pltpu.VMEM((6, 2, HALF, KH), BF16),
+        pltpu.VMEM((NB + 1, KH, BS), BF16),
+        pltpu.VMEM((NB + 1, 2, HALF, KH), BF16),
         pltpu.VMEM((2, KH, BS), BF16),
         pltpu.VMEM((2, 2, HALF, KH), BF16),
+        pltpu.VMEM((2, 2, HALF, BS), F32),
         pltpu.VMEM((LIVE_ROWS, LANES), F32),
         pltpu.VMEM((LIVE_ROWS, LANES), F32),
         pltpu.VMEM((LIVE_ROWS, LANES), F32),
@@ -384,10 +416,10 @@
         dma((NB + 2,)),
         dma((2,)),
         dma((2,)),
-        dma((NB,)),
-        dma((NB,)),
-        dma((6,)),
-        dma((6,)),
+        dma((NB + 1,)),
+        dma((NB + 1,)),
+        dma((NB + 2,)),
+        dma((NB + 2,)),
         dma((NSTAGE,)),
         dma((NSTAGE,)),
         dma((NSTAGE, NY - 1)),

time: 52.7 us -> 51.8 us (0.983)
  Pallas kernels: 51.7 us -> 50.8 us
    pallas_call x1, Pallas kernels: 51.7 us -> 50.8 us  [influence(): pl.pallas_call(kernel, out_shape=jax.ShapeDtypeStruct((PIECE, SLOTS, NB,...]
where the time goes in v4:
time: 51.8 us; the launch traced here: 51.7 us
  Pallas kernels  50.8 us (98%)
  local copies, waits for them, and re-layouts  0.93 us (2%)
    pallas_call x1, Pallas kernels, influence(): pl.pallas_call(kernel, out_shape=jax.ShapeDtypeStruct((PIECE, SLOTS, NB,...  50.8 us

profile of v4, /device:TPU:1, one launch (start us, length us, event | category | flops | bytes accessed | tf_op | source)
XLA Modules:
  0.0 51.7 jit_solution(17651051250812965596)
XLA Ops:
  0.0 50.8 %shard_map.37 = f32[32,7,4,256]{3,2,1,0:T(4,128)S(1)} custom-call(f32[768,1024]{1,0:T(8,128)} %bitcast.4, f32[768,64]{1,0:T(8,128)} %bitcast.5, s32[4,7]{1,0:T(4,128)} %partners_hbm.1), custom_call_target="tpu_custom_call" | custom-call | tf_op jit(solution)/shard_map/pallas_call | solution.py:430
  50.8 0.9 %copy.5 = f32[32,4,7,256]{3,1,2,0:T(4,128)} copy(f32[32,4,7,256]{3,1,2,0:T(4,128)S(1)} %bitcast.3) | data formatting | bytes 1835008

commit v5 on v4

--- a/solution.py
+++ b/solution.py
@@ -357,8 +357,8 @@
     left[2].wait_recv()
     right[2].wait_recv()
     compute(4)
+    presum(4)
     mixed_early()
-    presum(4)
     final(2)
     right[RX].wait_recv()
     mixed(1 - core)

time: 51.8 us -> 50.2 us (0.969)
  Pallas kernels: 50.8 us -> 49.1 us
    pallas_call x1, Pallas kernels: 50.8 us -> 49.1 us  [influence(): pl.pallas_call(kernel, out_shape=jax.ShapeDtypeStruct((PIECE, SLOTS, NB,...]
where the time goes in v5:
time: 50.2 us; the launch traced here: 50 us
  Pallas kernels  49.1 us (98%)
  local copies, waits for them, and re-layouts  0.93 us (2%)
    pallas_call x1, Pallas kernels, influence(): pl.pallas_call(kernel, out_shape=jax.ShapeDtypeStruct((PIECE, SLOTS, NB,...  49.1 us

profile of v5, /device:TPU:1, one launch (start us, length us, event | category | flops | bytes accessed | tf_op | source)
XLA Modules:
  0.0 50.0 jit_solution(4275170556711993999)
XLA Ops:
  0.0 49.1 %shard_map.37 = f32[32,7,4,256]{3,2,1,0:T(4,128)S(1)} custom-call(f32[768,1024]{1,0:T(8,128)} %bitcast.4, f32[768,64]{1,0:T(8,128)} %bitcast.5, s32[4,7]{1,0:T(4,128)} %partners_hbm.1), custom_call_target="tpu_custom_call" | custom-call | tf_op jit(solution)/shard_map/pallas_call | solution.py:430
  49.1 0.9 %copy.5 = f32[32,4,7,256]{3,1,2,0:T(4,128)} copy(f32[32,4,7,256]{3,1,2,0:T(4,128)S(1)} %bitcast.3) | data formatting | bytes 1835008

commit v6 on v5

--- a/solution.py
+++ b/solution.py
@@ -357,8 +357,9 @@
     left[2].wait_recv()
     right[2].wait_recv()
     compute(4)
+    pl.when(core == 1)(mixed_early)
     presum(4)
-    mixed_early()
+    pl.when(core == 0)(mixed_early)
     final(2)
     right[RX].wait_recv()
     mixed(1 - core)

time: 50.2 us -> 50.7 us (level)
    pallas_call x1, Pallas kernels: 49.1 us -> 49.6 us  [influence(): pl.pallas_call(kernel, out_shape=jax.ShapeDtypeStruct((PIECE, SLOTS, NB,...]
where the time goes in v6:
time: 50.7 us; the launch traced here: 50.6 us
  Pallas kernels  49.6 us (98%)
  local copies, waits for them, and re-layouts  0.93 us (2%)
    pallas_call x1, Pallas kernels, influence(): pl.pallas_call(kernel, out_shape=jax.ShapeDtypeStruct((PIECE, SLOTS, NB,...  49.6 us

profile of v6, /device:TPU:1, one launch (start us, length us, event | category | flops | bytes accessed | tf_op | source)
XLA Modules:
  0.0 50.6 jit_solution(549259935838216834)
XLA Ops:
  0.0 49.6 %shard_map.37 = f32[32,7,4,256]{3,2,1,0:T(4,128)S(1)} custom-call(f32[768,1024]{1,0:T(8,128)} %bitcast.4, f32[768,64]{1,0:T(8,128)} %bitcast.5, s32[4,7]{1,0:T(4,128)} %partners_hbm.1), custom_call_target="tpu_custom_call" | custom-call | tf_op jit(solution)/shard_map/pallas_call | solution.py:431
  49.7 0.9 %copy.5 = f32[32,4,7,256]{3,1,2,0:T(4,128)} copy(f32[32,4,7,256]{3,1,2,0:T(4,128)S(1)} %bitcast.3) | data formatting | bytes 1835008
